TPU v7x, 32 devices: a whole 2x2x4 slice. The times are simulated.
32 devices in a mesh: ta: 4 (over y, x), gz: 2 (over core), xy: 4 (over z).
Axes of the slice: x: 2, y: 2, z: 4, core: 2. Of those that a mesh axis runs over, the one named last changes fastest.
Arguments:
- source: float32 [2, 4, 3, 16, 16, 512], P(None, None, None, 'ta', 'gz', 'xy'), may hold values from -6 to 6
- iterate: float32 [2, 4, 3, 16, 16, 512], P(None, None, None, 'ta', 'gz', 'xy'), may hold values from -6 to 6
- gauge_links: float32 [4, 2, 3, 3, 16, 16, 512], P(None, None, None, None, 'ta', 'gz', 'xy'), may hold values from -2.4 to 2.4
- clover: float32 [2, 2, 6, 6, 16, 16, 512], P(None, None, None, None, 'ta', 'gz', 'xy'), may hold values from -0.6 to 0.6
- bc_sign: int32 [4], replicated, may hold values from -1 to 1, as said below
- null_store: bfloat16 [4, 4, 4, 2, 24, 12, 4, 4, 128], P('ta', 'gz', 'xy'), may hold values from -0.109375 to 0.109375
- block_slot: int32 [4, 4, 4], P('ta', 'gz', 'xy'), may hold values from 0 to 1, as said below
- coarse_links: float32 [9, 2, 24, 24, 4, 4, 4, 8], P(None, None, None, None, 'ta', 'gz', 'xy'), may hold values from -0.2 to 0.2
Outputs:
- new_iterate: float32 [2, 4, 3, 16, 16, 512], P(None, None, None, 'ta', 'gz', 'xy')
- new_residual: float32 [2, 4, 3, 16, 16, 512], P(None, None, None, 'ta', 'gz', 'xy')
Inputs may be any that keep to these rules, and one draw needn't show every extreme that they name: `bc_sign`: each entry is -1 or +1. `block_slot`: within each device's block of 2 aggregate columns the entries are the numbers 0 to 1, each once.
All inputs are finite; a program needn't handle non-finite values.
Results may differ from a plain program's by a relative error of at most 0.0016.
Values sent between devices are 32-bit elements; how exact they have to be, the bound alone decides.
A program may use at most 256 MiB of HBM per device.

v0:
```python
import jax
import jax.numpy as jnp
import numpy as np
from jax import lax
from jax.sharding import PartitionSpec as P

BLK = 4
LY = 32
CITERS = 4


MASS_TERM = 3.8
RELAX_WEIGHT = 0.4
HIGHEST = lax.Precision.HIGHEST


def padded_2(block, sides, width):
    for axis, dim in sides:
        count = lax.axis_size(axis)
        forward = [(i, i + 1) for i in range(count - 1)]
        forward.append((count - 1, 0))
        backward = [(target, source) for source, target in forward]
        low = lax.ppermute(
            lax.slice_in_dim(block, block.shape[dim] - width, None, axis=dim), axis, forward
        )
        high = lax.ppermute(lax.slice_in_dim(block, 0, width, axis=dim), axis, backward)
        block = jnp.concatenate([low, block, high], axis=dim)
    return block


def from_behind(value, axis, by):
    count = lax.axis_size(axis)
    return lax.ppermute(value, axis, [(i, (i + by) % count) for i in range(count)])


def chiral_blocks():
    identity = np.eye(2)
    nought = np.zeros((2, 2))
    flip_x = np.array([[0.0, 1.0], [1.0, 0.0]])
    flip_z = np.array([[1.0, 0.0], [0.0, -1.0]])
    rotate = np.array([[0.0, -1.0], [1.0, 0.0]])
    return [(identity, nought), (nought, -flip_z), (nought, -flip_x), (rotate, nought)]


def four_square(top_left, top_right, bottom_left, bottom_right):
    upper = np.concatenate([top_left, top_right], axis=1)
    lower = np.concatenate([bottom_left, bottom_right], axis=1)
    return np.concatenate([upper, lower], axis=0)


def spin_tables(direction, parity):
    upper_re, upper_im = chiral_blocks()[direction]
    identity = np.eye(2)
    nought = np.zeros((2, 2))
    gamma_re = four_square(nought, upper_re, upper_re.T, nought)
    gamma_im = four_square(nought, upper_im, -upper_im.T, nought)
    whole_re = np.eye(4) + parity * gamma_re
    whole_im = parity * gamma_im
    half_re = np.concatenate([identity, parity * upper_re], axis=1)
    half_im = np.concatenate([nought, parity * upper_im], axis=1)
    back_re = np.concatenate([identity, parity * upper_re.T], axis=0)
    back_im = np.concatenate([nought, -parity * upper_im.T], axis=0)
    return [
        np.asarray(matrix, np.float32)
        for matrix in (whole_re, whole_im, half_re, half_im, back_re, back_im)
    ]


def spin_times(matrix_re, matrix_im, field):
    real_part = jnp.tensordot(matrix_re, field[0], axes=(1, 0), precision=HIGHEST) - jnp.tensordot(
        matrix_im, field[1], axes=(1, 0), precision=HIGHEST
    )
    imag_part = jnp.tensordot(matrix_re, field[1], axes=(1, 0), precision=HIGHEST) + jnp.tensordot(
        matrix_im, field[0], axes=(1, 0), precision=HIGHEST
    )
    return jnp.stack([real_part, imag_part])


def colour_times(link, field):
    real_part = 0.0
    imag_part = 0.0
    for column in range(3):
        link_re = link[0][:, column][None]
        link_im = link[1][:, column][None]
        field_re = field[0][:, column : column + 1]
        field_im = field[1][:, column : column + 1]
        real_part = real_part + link_re * field_re - link_im * field_im
        imag_part = imag_part + link_re * field_im + link_im * field_re
    return jnp.stack([real_part, imag_part])


def colour_dagger(link, field):
    real_part = 0.0
    imag_part = 0.0
    for column in range(3):
        link_re = link[0][column][None]
        link_im = link[1][column][None]
        field_re = field[0][:, column : column + 1]
        field_im = field[1][:, column : column + 1]
        real_part = real_part + link_re * field_re + link_im * field_im
        imag_part = imag_part + link_re * field_im - link_im * field_re
    return jnp.stack([real_part, imag_part])


def clover_times(clover, field):
    halves = []
    for chirality in range(2):
        chiral_part = field[:, 2 * chirality : 2 * chirality + 2]
        chiral_part = chiral_part.reshape((2, 6) + chiral_part.shape[3:])
        matrix_re = clover[chirality, 0]
        matrix_im = clover[chirality, 1]
        real_part = 0.0
        imag_part = 0.0
        for column in range(6):
            real_part = (
                real_part
                + matrix_re[:, column] * chiral_part[0, column][None]
                - matrix_im[:, column] * chiral_part[1, column][None]
            )
            imag_part = (
                imag_part
                + matrix_re[:, column] * chiral_part[1, column][None]
                + matrix_im[:, column] * chiral_part[0, column][None]
            )
        halves.append(jnp.stack([real_part, imag_part]).reshape((2, 2, 3) + chiral_part.shape[2:]))
    return jnp.concatenate(halves, axis=1)


def along_y(field, forward):
    column_y = jnp.arange(field.shape[-1], dtype=jnp.int32) % LY
    if forward:
        return jnp.where(
            column_y == LY - 1, jnp.roll(field, LY - 1, axis=-1), jnp.roll(field, -1, axis=-1)
        )
    return jnp.where(column_y == 0, jnp.roll(field, 1 - LY, axis=-1), jnp.roll(field, 1, axis=-1))


def edge_factors(bc_sign, shape):
    count_t, count_z, count_xy = shape
    rows_x = count_xy // LY
    flat_index = jnp.arange(count_xy, dtype=jnp.int32)
    place_t = lax.axis_index("ta") * count_t + jnp.arange(count_t, dtype=jnp.int32)
    place_z = lax.axis_index("gz") * count_z + jnp.arange(count_z, dtype=jnp.int32)
    place_x = lax.axis_index("xy") * rows_x + flat_index // LY
    places = [
        (place_t[:, None, None], count_t * lax.axis_size("ta")),
        (place_z[None, :, None], count_z * lax.axis_size("gz")),
        (place_x[None, None, :], rows_x * lax.axis_size("xy")),
        ((flat_index % LY)[None, None, :], LY),
    ]
    factors = []
    for direction in range(4):
        where_now, extent = places[direction]
        flipped = bc_sign[direction].astype(jnp.float32)
        factors.append(
            (
                jnp.where(where_now == extent - 1, flipped, 1.0),
                jnp.where(where_now == 0, flipped, 1.0),
            )
        )
    return factors


def fine_apply(field, gauge_links, clover, factors, links_below):
    result = MASS_TERM * field + clover_times(clover, field)
    row_width = LY
    slab_halo = padded_2(field, (("ta", 3), ("gz", 4)), 1)
    row_halo = padded_2(field, (("xy", 5),), row_width)
    forward = [
        slab_halo[:, :, :, 2:, 1:-1],
        slab_halo[:, :, :, 1:-1, 2:],
        row_halo[:, :, :, :, :, 2 * row_width :],
    ]
    backward = [
        slab_halo[:, :, :, :-2, 1:-1],
        slab_halo[:, :, :, 1:-1, :-2],
        row_halo[:, :, :, :, :, : -2 * row_width],
    ]
    for direction in range(3):
        minus_tables = spin_tables(direction, -1)
        plus_tables = spin_tables(direction, 1)
        ahead = colour_times(gauge_links[direction], forward[direction] * factors[direction][0])
        behind = colour_dagger(links_below[direction], backward[direction] * factors[direction][1])
        result = result - 0.5 * (
            spin_times(minus_tables[0], minus_tables[1], ahead)
            + spin_times(plus_tables[0], plus_tables[1], behind)
        )
    minus_tables = spin_tables(3, -1)
    plus_tables = spin_tables(3, 1)
    ahead = colour_times(gauge_links[3], along_y(field, True) * factors[3][0])
    behind = colour_dagger(along_y(gauge_links[3], False), along_y(field, False) * factors[3][1])
    result = result - 0.5 * (
        spin_times(minus_tables[0], minus_tables[1], ahead)
        + spin_times(plus_tables[0], plus_tables[1], behind)
    )
    return result


def restrict_local(rounded, null_rows):
    count_t, count_z, count_xy = rounded.shape[3:]
    width = BLK * LY
    grid_t, grid_z, grid_x = (count_t // BLK, count_z // BLK, count_xy // width)
    shaped = rounded.reshape((2, 12, grid_t, BLK, grid_z, BLK, grid_x, width))
    turned = jnp.stack([shaped[1], -shaped[0]])
    paired = jnp.stack([shaped, turned])
    coarse = jnp.einsum(
        "tzxpvsabw,qpstazbxw->qvtzxw", null_rows, paired, preferred_element_type=jnp.float32
    )
    coarse = coarse.reshape(coarse.shape[:5] + (BLK, LY // BLK, BLK))
    return coarse.sum(axis=(5, 7))


def prolong_local(coarse_round, null_rows, field_shape):
    width = BLK * LY
    spread = jnp.broadcast_to(
        coarse_round[..., None, :, None], coarse_round.shape[:5] + (BLK, LY // BLK, BLK)
    )
    spread = spread.reshape(coarse_round.shape[:5] + (width,))
    mixture = jnp.stack([jnp.stack([spread[0], -spread[1]]), jnp.stack([spread[1], spread[0]])])
    fine = jnp.einsum(
        "tzxpvsabw,qpvtzxw->qstazbxw", null_rows, mixture, preferred_element_type=jnp.float32
    )
    return fine.reshape(field_shape)


def block_times(block_links, stacked):
    links_re = block_links[:, 0]
    links_im = block_links[:, 1]
    vector_re = stacked[:, 0]
    vector_im = stacked[:, 1]
    real_part = jnp.einsum(
        "kijabcd,kjabcd->iabcd", links_re, vector_re, precision=HIGHEST
    ) - jnp.einsum("kijabcd,kjabcd->iabcd", links_im, vector_im, precision=HIGHEST)
    imag_part = jnp.einsum(
        "kijabcd,kjabcd->iabcd", links_re, vector_im, precision=HIGHEST
    ) + jnp.einsum("kijabcd,kjabcd->iabcd", links_im, vector_re, precision=HIGHEST)
    return jnp.stack([real_part, imag_part])


def stencil(vector, block_links, ahead_list, behind_list):
    neighbours = [
        vector,
        ahead_list[0],
        behind_list[0],
        ahead_list[1],
        behind_list[1],
        ahead_list[2],
        behind_list[2],
        jnp.roll(vector, -1, 5),
        jnp.roll(vector, 1, 5),
    ]
    return 2.0 * vector + block_times(block_links, jnp.stack(neighbours))


def coarse_spread(vector, block_links):
    padded = padded_2(vector, (("ta", 2), ("gz", 3), ("xy", 4)), 1)
    ahead_list = (
        padded[:, :, 2:, 1:-1, 1:-1],
        padded[:, :, 1:-1, 2:, 1:-1],
        padded[:, :, 1:-1, 1:-1, 2:],
    )
    behind_list = (
        padded[:, :, :-2, 1:-1, 1:-1],
        padded[:, :, 1:-1, :-2, 1:-1],
        padded[:, :, 1:-1, 1:-1, :-2],
    )
    return stencil(vector, block_links, ahead_list, behind_list)


def per_device(source, iterate, gauge_links, clover, bc_sign, null_store, block_slot, coarse_links):
    factors = edge_factors(bc_sign, source.shape[3:])
    time_face = from_behind(gauge_links[0][:, :, :, -1:], "ta", 1)
    depth_face = from_behind(gauge_links[1][:, :, :, :, -1:], "gz", 1)
    plane_face = from_behind(gauge_links[2][:, :, :, :, :, -LY:], "xy", 1)
    links_below = [
        jnp.concatenate([time_face, gauge_links[0][:, :, :, :-1]], axis=3),
        jnp.concatenate([depth_face, gauge_links[1][:, :, :, :, :-1]], axis=4),
        jnp.concatenate([plane_face, gauge_links[2][:, :, :, :, :, :-LY]], axis=5),
    ]
    residual_start = source - fine_apply(iterate, gauge_links, clover, factors, links_below)
    group_grid = null_store.shape[:3]
    flat_store = null_store.reshape((-1,) + null_store.shape[3:])
    null_rows = jnp.take(flat_store, block_slot.reshape(-1), axis=0)
    null_rows = null_rows.reshape(group_grid + null_rows.shape[1:])
    coarse_rhs = restrict_local(residual_start.astype(jnp.bfloat16), null_rows)
    coarse_sol = RELAX_WEIGHT * coarse_rhs
    for iteration in range(CITERS - 1):
        coarse_sol = coarse_sol + RELAX_WEIGHT * (
            coarse_rhs - coarse_spread(coarse_sol, coarse_links)
        )
    coarse_round = coarse_sol.astype(jnp.bfloat16)
    correction = prolong_local(coarse_round, null_rows, source.shape)
    new_iterate = iterate + correction
    new_residual = residual_start - fine_apply(
        correction, gauge_links, clover, factors, links_below
    )
    return (new_iterate, new_residual)


def solution(mesh):
    placed = (
        P(None, None, None, "ta", "gz", "xy"),
        P(None, None, None, "ta", "gz", "xy"),
        P(None, None, None, None, "ta", "gz", "xy"),
        P(None, None, None, None, "ta", "gz", "xy"),
        P(),
        P("ta", "gz", "xy", None, None, None, None, None, None),
        P("ta", "gz", "xy"),
        P(None, None, None, None, "ta", "gz", "xy", None),
    )
    return jax.shard_map(
        per_device,
        mesh=mesh,
        in_specs=placed,
        out_specs=(P(None, None, None, "ta", "gz", "xy"), P(None, None, None, "ta", "gz", "xy")),
        check_vma=False,
    )
```

profile of v0, /device:TPU:0, one launch (start us, length us, event | category | flops | bytes accessed | tf_op | source)
XLA Modules:
  0.0 480.4 jit_solution(9383578854027165756)
XLA Ops:
  0.6 1.7 fusion.169
  2.4 3.0 collective-permute-start.2
  6.3 2.1 fusion.170
  8.4 4.1 collective-permute-start.6
  31.6 11.3 %while.1 = (s32[]{:T(128)}, bf16[2,2,24,12,4,4,128]{6,5,4,3,2,1,0:T(4,128)(2,1)}, s32[2,1]{0,1:T(1,128)S(1)}, bf16[2,2,24,12,4,4,128]{6,5,4,3,2,1,0:T(4,128)(2,1)}, s32[]{:T(128)}) while((s32[]{:T(128)}, bf16[2,2,24,12,4,4,128]{6,5,4,3,2,1,0:T(4,128)(2,1)}, s32[2,1]{0,1:T(1,128)S(1)}, bf16[2,2,24,12,4,4,128]{6,5,4,3,2,1,0:T(4,128)(2,1)}, ...), condition=%wide.while_cond, body=%wide.while_body.sunk | while | flops 2 | bytes 4719689 | solution.py:283
  32.6 4.8 %dynamic-slice_dynamic-update-slice_fusion.2 = bf16[2,2,24,12,4,4,128]{6,5,4,3,2,1,0:T(4,128)(2,1)} fusion(bf16[2,2,24,12,4,4,128]{6,5,4,3,2,1,0:T(4,128)(2,1)} %get-tuple-element.475, s32[]{:T(128)} %get-tuple-element.472, bf16[2,2,24,12,4,4,128]{6,5,4,3,2,1,0:T(4,128)(2,1)} %get-tuple-element.478, s32[]{:T(128)} %bitcast.1238), kind=kLoop, calls=%fused_computation.clone.1 | loop fusion | bytes 4719616 | tf_op jit(solution)/shard_map/jit(_take)/gather
  38.0 4.9 %dynamic-slice_dynamic-update-slice_fusion.2 = bf16[2,2,24,12,4,4,128]{6,5,4,3,2,1,0:T(4,128)(2,1)} fusion(bf16[2,2,24,12,4,4,128]{6,5,4,3,2,1,0:T(4,128)(2,1)} %get-tuple-element.475, s32[]{:T(128)} %get-tuple-element.472, bf16[2,2,24,12,4,4,128]{6,5,4,3,2,1,0:T(4,128)(2,1)} %get-tuple-element.478, s32[]{:T(128)} %bitcast.1238), kind=kLoop, calls=%fused_computation.clone.1 | loop fusion | bytes 4719616 | tf_op jit(solution)/shard_map/jit(_take)/gather
  42.9 3.6 slice_bitcast_fusion
  54.8 6.6 %broadcast_select_fusion = bf16[2,2,24,12,4,4,128]{6,5,4,3,2,1,0:T(4,128)(2,1)} fusion(bf16[2,2,24,12,4,4,128]{6,5,4,3,2,1,0:T(4,128)(2,1)} %get-tuple-element.9, pred[2]{0:T(512)(128)(4,1)S(1)} %compare_and_fusion), kind=kLoop, calls=%fused_computation.2 | loop fusion | flops 2359296 | bytes 9437186 | tf_op jit(solution)/shard_map/jit(_take)/select_n | solution.py:283
  63.4 54.7 %copy.1550 = bf16[2,2,24,12,4,4,128]{2,3,1,5,6,0,4:T(8,128)(2,1)} copy(bf16[2,2,24,12,4,4,128]{6,5,4,3,2,1,0:T(4,128)(2,1)} %broadcast_select_fusion) | data formatting | bytes 9437184 | tf_op jit(solution)/shard_map/jit(_take)/select_n | solution.py:283
  118.1 54.7 %copy.1456 = bf16[2,2,24,12,4,4,128]{2,3,1,5,4,6,0:T(8,128)(2,1)} copy(bf16[2,2,24,12,4,4,128]{6,5,4,3,2,1,0:T(4,128)(2,1)} %broadcast_select_fusion) | data formatting | bytes 9437184 | tf_op jit(solution)/shard_map/jit(_take)/select_n | solution.py:283
  174.5 1.8 copy.1553
  178.0 4.1 collective-permute-done.1
  183.6 9.9 %collective-permute-done.7 = f32[2,3,3,4,8,32]{5,4,3,2,1,0:T(8,128)S(1)} collective-permute-done((f32[2,3,3,4,8,32]{5,4,3,2,1,0:T(8,128)}, f32[2,3,3,4,8,32]{5,4,3,2,1,0:T(8,128)S(1)}, u32[]{:S(2)}, u32[]{:S(2)}) %collective-permute-start.7) | collective-permute-done | bytes 73760 | tf_op jit(solution)/shard_map/ppermute | solution.py:33
  195.7 1.7 fusion.13
  219.3 9.8 %copy.1413 = bf16[1,2,12,1,4,2,4,1,128]{2,0,1,6,5,8,4,7,3:T(2,128)(2,1)} copy(bf16[1,2,12,1,4,2,4,1,128]{8,6,5,4,2,1,7,3,0:T(4,128)(2,1)} %maximum_bitcast_fusion.1) | data formatting | bytes 393216 | tf_op jit(solution)/shard_map/stack | solution.py:205
  229.2 9.8 %copy.1412 = bf16[1,2,12,1,4,2,4,1,128]{2,0,1,6,5,8,4,7,3:T(2,128)(2,1)} copy(bf16[1,2,12,1,4,2,4,1,128]{8,6,5,4,2,1,7,3,0:T(4,128)(2,1)} %bitcast.1350) | data formatting | bytes 393216 | tf_op jit(solution)/shard_map/stack;reshape | solution.py:205
  238.9 29.4 %fusion = f32[2,128,2,24,1,1,1]{3,2,6,5,1,0,4:T(2,128)} fusion(bf16[2,2,24,12,4,4,128]{2,3,1,5,6,0,4:T(8,128)(2,1)} %copy.1550, bf16[1,2,12,1,4,2,4,1,128]{2,0,1,6,5,8,4,7,3:T(2,128)(2,1)} %copy.1413, bf16[1,2,12,1,4,2,4,1,128]{2,0,1,6,5,8,4,7,3:T(2,128)(2,1)} %copy.1412), kind=kOutput, calls=%fused_computation.4 | convolution fusion | flops 10223616 | bytes 5160960 | tf_op jit(solution)/shard_map/tzxpvsabw,qpstazbxw->qvtzxw/dot_general | solution.py:206
  268.3 1.7 copy.1551
  271.2 2.9 collective-permute-start.9
  274.2 1.7 collective-permute-done.10
  277.5 1.8 collective-permute-start.13
  279.8 2.8 collective-permute-done.13
  282.6 3.4 collective-permute-done.14
  286.1 1.7 fusion.120
  287.9 1.7 fusion.122
  289.6 1.7 fusion.124
  291.3 1.7 fusion.118
  293.1 2.7 collective-permute-start.15
  297.6 2.9 collective-permute-done.16
  304.4 2.6 collective-permute-done.19
  307.0 2.7 collective-permute-done.20
  309.7 1.7 fusion.116
  311.5 1.7 fusion.114
  313.2 1.7 fusion.112
  314.9 1.7 fusion.110
  317.0 1.8 collective-permute-start.22
  325.3 2.9 collective-permute-done.25
  328.2 3.0 collective-permute-done.26
  331.2 1.7 fusion.108
  332.9 1.7 fusion.106
  334.7 1.7 fusion.104
  336.4 1.7 fusion.102
  338.7 84.2 %convolution_bitcast_fusion = f32[2,12,1,4,2,4,1,128]{1,0,5,3,7,4,6,2:T(2,128)} fusion(bf16[2,2,24,12,4,4,128]{2,3,1,5,4,6,0:T(8,128)(2,1)} %copy.1456, bf16[2,2,24,1,2,1,128]{2,0,1,6,4,5,3:T(2,128)(2,1)S(1)} %copy.1455), kind=kOutput, calls=%fused_computation.6 | convolution fusion | flops 9437184 | bytes 5160960 | tf_op jit(solution)/shard_map/tzxpvsabw,qpvtzxw->qstazbxw/dot_general | solution.py:220
  422.9 5.6 %copy.1457 = f32[2,12,1,4,2,4,1,128]{7,5,4,3,1,0,6,2:T(4,128)S(1)} copy(f32[2,12,1,4,2,4,1,128]{1,0,5,3,7,4,6,2:T(2,128)} %convolution_bitcast_fusion) | data formatting | bytes 786432 | tf_op jit(solution)/shard_map/tzxpvsabw,qpvtzxw->qstazbxw/transpose | solution.py:220
  437.4 1.9 collective-permute-start.27
  439.9 3.8 collective-permute-start.31
  443.9 14.7 %collective-permute-done.31 = f32[2,4,3,4,8,32]{5,4,3,2,1,0:T(8,128)S(1)} collective-permute-done((f32[2,4,3,4,8,32]{5,4,3,2,1,0:T(8,128)S(1)}, f32[2,4,3,4,8,32]{5,4,3,2,1,0:T(8,128)S(1)}, u32[]{:S(2)}, u32[]{:S(2)}) %collective-permute-start.31) | collective-permute-done | bytes 98336 | tf_op jit(solution)/shard_map/ppermute | solution.py:26
  (861 shorter events, 100.6 us)
Async XLA Ops:
  2.4 192.3 %collective-permute-start.2 = (f32[2,4,3,1,8,128]{5,4,3,2,1,0:T(8,128)}, f32[2,4,3,1,8,128]{5,4,3,2,1,0:T(8,128)}, u32[]{:S(2)}, u32[]{:S(2)}) collective-permute-start(f32[2,4,3,1,8,128]{5,4,3,2,1,0:T(8,128)} %get-tuple-element.171), channel_id=1, source_target_pairs={{0,8},{8,16},{16,24},{24,0},{1,9},{9,17},{17,25},{25,1},{2,10},{10... | collective-permute-start | bytes 294920 | tf_op jit(solution)/shard_map/ppermute | solution.py:23
  5.3 190.3 %collective-permute-start = (f32[2,4,3,1,8,128]{5,4,3,2,1,0:T(8,128)}, f32[2,4,3,1,8,128]{5,4,3,2,1,0:T(8,128)}, u32[]{:S(2)}, u32[]{:S(2)}) collective-permute-start(f32[2,4,3,1,8,128]{5,4,3,2,1,0:T(8,128)} %get-tuple-element.170), channel_id=1, source_target_pairs={{8,0},{16,8},{24,16},{0,24},{9,1},{17,9},{25,17},{1,25},{10,2},{18... | collective-permute-start | bytes 294920 | tf_op jit(solution)/shard_map/ppermute | solution.py:26
  8.4 187.2 %collective-permute-start.6 = (f32[2,4,3,4,8,32]{5,4,3,2,1,0:T(8,128)}, f32[2,4,3,4,8,32]{5,4,3,2,1,0:T(8,128)}, u32[]{:S(2)}, u32[]{:S(2)}) collective-permute-start(f32[2,4,3,4,8,32]{5,4,3,2,1,0:T(8,128)} %get-tuple-element.174), channel_id=1, source_target_pairs={{1,0},{2,1},{3,2},{0,3},{5,4},{6,5},{7,6},{4,7},{9,8},{10,9},{11,1... | collective-permute-start | bytes 294920 | tf_op jit(solution)/shard_map/ppermute | solution.py:26
  12.5 183.1 %collective-permute-start.8 = (f32[2,4,3,4,8,32]{5,4,3,2,1,0:T(8,128)}, f32[2,4,3,4,8,32]{5,4,3,2,1,0:T(8,128)}, u32[]{:S(2)}, u32[]{:S(2)}) collective-permute-start(f32[2,4,3,4,8,32]{5,4,3,2,1,0:T(8,128)} %get-tuple-element.175), channel_id=1, source_target_pairs={{0,1},{1,2},{2,3},{3,0},{4,5},{5,6},{6,7},{7,4},{8,9},{9,10},{10,1... | collective-permute-start | bytes 294920 | tf_op jit(solution)/shard_map/ppermute | solution.py:23
  14.8 161.5 %collective-permute-start.4 = (f32[2,3,3,4,1,128]{5,4,3,2,1,0:T(1,128)}, f32[2,3,3,4,1,128]{5,4,3,2,1,0:T(1,128)}, u32[]{:S(2)}, u32[]{:S(2)}) collective-permute-start(f32[2,3,3,4,1,128]{5,4,3,2,1,0:T(1,128)} %slice.2031), channel_id=1, source_target_pairs={{0,4},{4,0},{1,5},{5,1},{2,6},{6,2},{3,7},{7,3},{8,12},{12,8},{9,1... | collective-permute-start | bytes 110600 | tf_op jit(solution)/shard_map/ppermute | solution.py:33
  46.5 149.1 %copy-start.190 = (f32[4]{0:T(128)}, f32[4]{0:T(128)S(1)}, u32[]{:S(2)}) copy-start(f32[4]{0:T(128)S(1)} %get-tuple-element.432) | copy-start | bytes 52
  46.5 149.1 %copy-start.192 = (f32[4]{0:T(128)}, f32[4]{0:T(128)S(1)}, u32[]{:S(2)}) copy-start(f32[4]{0:T(128)S(1)} %get-tuple-element.433) | copy-start | bytes 52
  118.1 54.8 %copy-start.4 = (f32[2,3,3,4,8,128]{5,4,3,2,1,0:T(8,128)S(1)}, f32[2,3,3,4,8,128]{5,4,3,2,1,0:T(8,128)}, u32[]{:S(2)}) copy-start(f32[2,3,3,4,8,128]{5,4,3,2,1,0:T(8,128)} %get-tuple-element.47) | copy-start | bytes 884740
  176.3 5.8 %collective-permute-start.1 = (f32[2,3,3,1,8,128]{5,4,3,2,1,0:T(8,128)}, f32[2,3,3,1,8,128]{5,4,3,2,1,0:T(8,128)S(1)}, u32[]{:S(2)}, u32[]{:S(2)}) collective-permute-start(f32[2,3,3,1,8,128]{5,4,3,2,1,0:T(8,128)} %slice.1996), channel_id=1, source_target_pairs={{0,8},{8,16},{16,24},{24,0},{1,9},{9,17},{17,25},{25,1},{2,10},{10... | collective-permute-start | bytes 221192 | tf_op jit(solution)/shard_map/ppermute | solution.py:33
  178.0 36.0 %copy-start.102 = (f32[3,4,8,128]{3,2,1,0:T(8,128)}, f32[3,4,8,128]{3,2,1,0:T(8,128)S(1)}, u32[]{:S(2)}) copy-start(f32[3,4,8,128]{3,2,1,0:T(8,128)S(1)} %get-tuple-element.190) | copy-start | bytes 147460
  178.0 36.0 %copy-start.104 = (f32[3,4,8,128]{3,2,1,0:T(8,128)}, f32[3,4,8,128]{3,2,1,0:T(8,128)S(1)}, u32[]{:S(2)}) copy-start(f32[3,4,8,128]{3,2,1,0:T(8,128)S(1)} %get-tuple-element.191) | copy-start | bytes 147460
  178.0 36.0 %copy-start.106 = (f32[3,4,8,128]{3,2,1,0:T(8,128)}, f32[3,4,8,128]{3,2,1,0:T(8,128)S(1)}, u32[]{:S(2)}) copy-start(f32[3,4,8,128]{3,2,1,0:T(8,128)S(1)} %get-tuple-element.192) | copy-start | bytes 147460
  178.0 36.0 %copy-start.108 = (f32[3,4,8,128]{3,2,1,0:T(8,128)}, f32[3,4,8,128]{3,2,1,0:T(8,128)S(1)}, u32[]{:S(2)}) copy-start(f32[3,4,8,128]{3,2,1,0:T(8,128)S(1)} %get-tuple-element.193) | copy-start | bytes 147460
  178.0 36.0 %copy-start.110 = (f32[3,4,8,128]{3,2,1,0:T(8,128)}, f32[3,4,8,128]{3,2,1,0:T(8,128)S(1)}, u32[]{:S(2)}) copy-start(f32[3,4,8,128]{3,2,1,0:T(8,128)S(1)} %get-tuple-element.194) | copy-start | bytes 147460
  178.0 36.0 %copy-start.112 = (f32[3,4,8,128]{3,2,1,0:T(8,128)}, f32[3,4,8,128]{3,2,1,0:T(8,128)S(1)}, u32[]{:S(2)}) copy-start(f32[3,4,8,128]{3,2,1,0:T(8,128)S(1)} %get-tuple-element.195) | copy-start | bytes 147460
  182.2 11.4 %collective-permute-start.7 = (f32[2,3,3,4,8,32]{5,4,3,2,1,0:T(8,128)}, f32[2,3,3,4,8,32]{5,4,3,2,1,0:T(8,128)S(1)}, u32[]{:S(2)}, u32[]{:S(2)}) collective-permute-start(f32[2,3,3,4,8,32]{5,4,3,2,1,0:T(8,128)} %slice.2066), channel_id=1, source_target_pairs={{0,1},{1,2},{2,3},{3,0},{4,5},{5,6},{6,7},{7,4},{8,9},{9,10},{10,1... | collective-permute-start | bytes 221192 | tf_op jit(solution)/shard_map/ppermute | solution.py:33
  183.6 19.7 %copy-start.90 = (f32[3,4,8,128]{3,2,1,0:T(8,128)}, f32[3,4,8,128]{3,2,1,0:T(8,128)S(1)}, u32[]{:S(2)}) copy-start(f32[3,4,8,128]{3,2,1,0:T(8,128)S(1)} %get-tuple-element.196) | copy-start | bytes 147460
  183.6 19.7 %copy-start.92 = (f32[3,4,8,128]{3,2,1,0:T(8,128)}, f32[3,4,8,128]{3,2,1,0:T(8,128)S(1)}, u32[]{:S(2)}) copy-start(f32[3,4,8,128]{3,2,1,0:T(8,128)S(1)} %get-tuple-element.197) | copy-start | bytes 147460
  183.6 19.7 %copy-start.94 = (f32[3,4,8,128]{3,2,1,0:T(8,128)}, f32[3,4,8,128]{3,2,1,0:T(8,128)S(1)}, u32[]{:S(2)}) copy-start(f32[3,4,8,128]{3,2,1,0:T(8,128)S(1)} %get-tuple-element.198) | copy-start | bytes 147460
  183.6 19.7 %copy-start.96 = (f32[3,4,8,128]{3,2,1,0:T(8,128)}, f32[3,4,8,128]{3,2,1,0:T(8,128)S(1)}, u32[]{:S(2)}) copy-start(f32[3,4,8,128]{3,2,1,0:T(8,128)S(1)} %get-tuple-element.199) | copy-start | bytes 147460
  209.1 1.3 collective-permute-start.3
  209.2 1.4 collective-permute-start.5
  271.2 4.7 collective-permute-start.10
  271.2 4.9 %collective-permute-start.9 = (f32[2,24,1,2,1,8]{1,5,3,0,4,2:T(8,128)S(1)}, f32[2,24,1,2,1,8]{1,5,3,0,4,2:T(8,128)S(1)}, u32[]{:S(2)}, u32[]{:S(2)}) collective-permute-start(f32[2,24,1,2,1,8]{1,5,3,0,4,2:T(8,128)S(1)} %bitcast_multiply_fusion.1), channel_id=1, source_target_pairs={{8,0},{16,8},{24,16},{0,24},{9,1},{17,9},{25,17},{1,25},{10,2},{18... | collective-permute-start | bytes 9224 | tf_op jit(solution)/shard_map/ppermute | solution.py:26
  276.1 1.3 collective-permute-start.11
  276.2 1.3 collective-permute-start.12
  277.5 5.1 %collective-permute-start.13 = (f32[2,24,3,4,1,8]{1,5,3,0,4,2:T(8,128)S(1)}, f32[2,24,3,4,1,8]{1,5,3,0,4,2:T(8,128)S(1)}, u32[]{:S(2)}, u32[]{:S(2)}) collective-permute-start(f32[2,24,3,4,1,8]{1,5,3,0,4,2:T(8,128)S(1)} %pad_maximum_fusion.16), channel_id=1, source_target_pairs={{1,0},{2,1},{3,2},{0,3},{5,4},{6,5},{7,6},{4,7},{9,8},{10,9},{11,1... | collective-permute-start | bytes 55304 | tf_op jit(solution)/shard_map/ppermute | solution.py:26
  279.3 6.8 %collective-permute-start.14 = (f32[2,24,3,4,1,8]{1,5,3,0,4,2:T(8,128)S(1)}, f32[2,24,3,4,1,8]{1,5,3,0,4,2:T(8,128)S(1)}, u32[]{:S(2)}, u32[]{:S(2)}) collective-permute-start(f32[2,24,3,4,1,8]{1,5,3,0,4,2:T(8,128)S(1)} %pad_maximum_fusion.16), channel_id=1, source_target_pairs={{0,1},{1,2},{2,3},{3,0},{4,5},{5,6},{6,7},{7,4},{8,9},{9,10},{10,1... | collective-permute-start | bytes 55304 | tf_op jit(solution)/shard_map/ppermute | solution.py:23
  293.1 4.5 collective-permute-start.15
  295.8 4.6 collective-permute-start.16
  300.5 1.3 collective-permute-start.17
  300.5 1.3 collective-permute-start.18
  301.9 5.1 %collective-permute-start.19 = (f32[2,24,3,4,1,8]{1,5,3,0,4,2:T(8,128)S(1)}, f32[2,24,3,4,1,8]{1,5,3,0,4,2:T(8,128)S(1)}, u32[]{:S(2)}, u32[]{:S(2)}) collective-permute-start(f32[2,24,3,4,1,8]{1,5,3,0,4,2:T(8,128)S(1)} %pad_maximum_fusion.17), channel_id=1, source_target_pairs={{1,0},{2,1},{3,2},{0,3},{5,4},{6,5},{7,6},{4,7},{9,8},{10,9},{11,1... | collective-permute-start | bytes 55304 | tf_op jit(solution)/shard_map/ppermute | solution.py:26
  302.7 6.9 %collective-permute-start.20 = (f32[2,24,3,4,1,8]{1,5,3,0,4,2:T(8,128)S(1)}, f32[2,24,3,4,1,8]{1,5,3,0,4,2:T(8,128)S(1)}, u32[]{:S(2)}, u32[]{:S(2)}) collective-permute-start(f32[2,24,3,4,1,8]{1,5,3,0,4,2:T(8,128)S(1)} %pad_maximum_fusion.17), channel_id=1, source_target_pairs={{0,1},{1,2},{2,3},{3,0},{4,5},{5,6},{6,7},{7,4},{8,9},{9,10},{10,1... | collective-permute-start | bytes 55304 | tf_op jit(solution)/shard_map/ppermute | solution.py:23
  316.7 3.8 collective-permute-start.21
  317.0 4.6 collective-permute-start.22
  321.6 1.3 collective-permute-start.23
  321.7 1.3 collective-permute-start.24
  323.1 5.1 %collective-permute-start.25 = (f32[2,24,3,4,1,8]{1,5,3,0,4,2:T(8,128)S(1)}, f32[2,24,3,4,1,8]{1,5,3,0,4,2:T(8,128)S(1)}, u32[]{:S(2)}, u32[]{:S(2)}) collective-permute-start(f32[2,24,3,4,1,8]{1,5,3,0,4,2:T(8,128)S(1)} %pad_maximum_fusion.18), channel_id=1, source_target_pairs={{1,0},{2,1},{3,2},{0,3},{5,4},{6,5},{7,6},{4,7},{9,8},{10,9},{11,1... | collective-permute-start | bytes 55304 | tf_op jit(solution)/shard_map/ppermute | solution.py:26
  324.4 6.7 %collective-permute-start.26 = (f32[2,24,3,4,1,8]{1,5,3,0,4,2:T(8,128)S(1)}, f32[2,24,3,4,1,8]{1,5,3,0,4,2:T(8,128)S(1)}, u32[]{:S(2)}, u32[]{:S(2)}) collective-permute-start(f32[2,24,3,4,1,8]{1,5,3,0,4,2:T(8,128)S(1)} %pad_maximum_fusion.18), channel_id=1, source_target_pairs={{0,1},{1,2},{2,3},{3,0},{4,5},{5,6},{6,7},{7,4},{8,9},{9,10},{10,1... | collective-permute-start | bytes 55304 | tf_op jit(solution)/shard_map/ppermute | solution.py:23
  437.1 21.5 %copy-start.2 = (f32[2,4,3,4,8,128]{5,4,3,2,1,0:T(8,128)S(1)}, f32[2,4,3,4,8,128]{5,4,3,2,1,0:T(8,128)}, u32[]{:S(2)}) copy-start(f32[2,4,3,4,8,128]{5,4,3,2,1,0:T(8,128)} %param.73) | copy-start | bytes 1179652
  437.1 21.5 %copy-start.199 = (f32[128]{0:T(128)S(1)}, f32[128]{0:T(128)}, u32[]{:S(2)}) copy-start(f32[128]{0:T(128)} %get-tuple-element.435) | copy-start | bytes 1540
  437.4 24.9 %collective-permute-start.27 = (f32[2,4,3,1,8,128]{5,4,3,2,1,0:T(8,128)S(1)}, f32[2,4,3,1,8,128]{5,4,3,2,1,0:T(8,128)S(1)}, u32[]{:S(2)}, u32[]{:S(2)}) collective-permute-start(f32[2,4,3,1,8,128]{5,4,3,2,1,0:T(8,128)S(1)} %get-tuple-element.150), channel_id=1, source_target_pairs={{8,0},{16,8},{24,16},{0,24},{9,1},{17,9},{25,17},{1,25},{10,2},{18... | collective-permute-start | bytes 294920 | tf_op jit(solution)/shard_map/ppermute | solution.py:26
  439.3 23.0 %collective-permute-start.28 = (f32[2,4,3,1,8,128]{5,4,3,2,1,0:T(8,128)S(1)}, f32[2,4,3,1,8,128]{5,4,3,2,1,0:T(8,128)S(1)}, u32[]{:S(2)}, u32[]{:S(2)}) collective-permute-start(f32[2,4,3,1,8,128]{5,4,3,2,1,0:T(8,128)S(1)} %get-tuple-element.149), channel_id=1, source_target_pairs={{0,8},{8,16},{16,24},{24,0},{1,9},{9,17},{17,25},{25,1},{2,10},{10... | collective-permute-start | bytes 294920 | tf_op jit(solution)/shard_map/ppermute | solution.py:23
  439.4 23.6 %collective-permute-start.32 = (f32[2,4,3,4,8,32]{5,4,3,2,1,0:T(8,128)S(1)}, f32[2,4,3,4,8,32]{5,4,3,2,1,0:T(8,128)S(1)}, u32[]{:S(2)}, u32[]{:S(2)}) collective-permute-start(f32[2,4,3,4,8,32]{5,4,3,2,1,0:T(8,128)S(1)} %get-tuple-element.137), channel_id=1, source_target_pairs={{0,1},{1,2},{2,3},{3,0},{4,5},{5,6},{6,7},{7,4},{8,9},{9,10},{10,1... | collective-permute-start | bytes 294920 | tf_op jit(solution)/shard_map/ppermute | solution.py:23
  439.9 18.6 %collective-permute-start.31 = (f32[2,4,3,4,8,32]{5,4,3,2,1,0:T(8,128)S(1)}, f32[2,4,3,4,8,32]{5,4,3,2,1,0:T(8,128)S(1)}, u32[]{:S(2)}, u32[]{:S(2)}) collective-permute-start(f32[2,4,3,4,8,32]{5,4,3,2,1,0:T(8,128)S(1)} %get-tuple-element.138), channel_id=1, source_target_pairs={{1,0},{2,1},{3,2},{0,3},{5,4},{6,5},{7,6},{4,7},{9,8},{10,9},{11,1... | collective-permute-start | bytes 294920 | tf_op jit(solution)/shard_map/ppermute | solution.py:26
  462.4 1.3 collective-permute-start.29
  462.5 1.4 collective-permute-start.30
  (192 other events, 603.1 us)
where the time goes:
time: 490 us; the launch traced here: 480 us
  local copies, waits for them, and re-layouts  183 us (37%)
  matrix products  164 us (33%)
  waiting for transfers between devices  59.2 us (12%)
  starting transfers between devices  33.2 us (7%)
  other arithmetic  32.3 us (7%)
  between operations  8.81 us (2%)
    select_n x2, local copies, waits for them, and re-layouts, per_device(): null_rows = jnp.take(flat_store, block_slot.reshape(-1), axis=0)  109 us
    dot_general x1, matrix products, prolong_local(): jnp.einsum('tzxpvsabw,qpvtzxw->qstazbxw', null_rows, mixture, preferred_e...  84.2 us
    ppermute x15, waiting for transfers between devices, padded_2(): lax.ppermute(lax.slice_in_dim(block, 0, width, axis=dim), axis, backward)  29.6 us
    dot_general x1, matrix products, restrict_local(): jnp.einsum('tzxpvsabw,qpstazbxw->qvtzxw', null_rows, paired, preferred_el...  29.4 us
    ppermute x15, starting transfers between devices, padded_2(): lax.ppermute(lax.slice_in_dim(block, 0, width, axis=dim), axis, backward)  21 us
    another operation x2, local copies, waits for them, and re-layouts, restrict_local(): paired = jnp.stack([shaped, turned])  19.6 us
    ppermute x15, waiting for transfers between devices, padded_2(): lax.ppermute(lax.slice_in_dim(block, block.shape[dim] - width, None, axis...  15.6 us
    ppermute x3, waiting for transfers between devices, from_behind(): lax.ppermute(value, axis, [(i, (i + by) % count) for i in range(count)])  14 us
  transfers between devices with their start and end apart: 33, of which 25 were waited for; matrix products, arithmetic and copies ran while one was open for 35% of the time, Pallas kernels for 0%

commit v1 on v0

v1 whole, which is shorter than its diff:
```python
import functools

import jax
import jax.numpy as jnp
from jax import lax
from jax.experimental import pallas as pl
from jax.experimental.pallas import tpu as pltpu
from jax.sharding import PartitionSpec as P

BLK = 4
LY = 32
CITERS = 4
MASS_TERM = 3.8
RELAX_WEIGHT = 0.4
HIGHEST = lax.Precision.HIGHEST
MESH = pl.DeviceIdType.MESH
F32 = jnp.float32

UPPER = [((0, 0), (1, 0)), ((0, 3), (1, 1)), ((1, 3), (0, 3)), ((1, 2), (0, 0))]
LOWER = [((0, 0), (1, 0)), ((0, 1), (1, 3)), ((1, 1), (0, 1)), ((1, 0), (0, 2))]


def add_turned(a, b, power):
    power %= 4
    if power == 0:
        return (a[0] + b[0], a[1] + b[1])
    if power == 1:
        return (a[0] - b[1], a[1] + b[0])
    if power == 2:
        return (a[0] - b[0], a[1] - b[1])
    return (a[0] + b[1], a[1] - b[0])


def project(psi, mu, forward):
    turn = 2 if forward else 0
    return [
        [add_turned(psi[row][c], psi[2 + UPPER[mu][row][0]][c], UPPER[mu][row][1] + turn) for c in range(3)]
        for row in range(2)
    ]


def rebuild(total, half, mu, forward):
    turn = 2 if forward else 0
    for row in range(2):
        index, power = LOWER[mu][row]
        for c in range(3):
            total[row][c] = add_turned(total[row][c], half[row][c], 0)
            total[2 + row][c] = add_turned(total[2 + row][c], half[index][c], power + turn)


def link_times(gauge, mu, t, half):
    out = [[None] * 3 for _ in range(2)]
    for a in range(3):
        for b in range(3):
            ur = gauge[mu, 0, a * 3 + b, t]
            ui = gauge[mu, 1, a * 3 + b, t]
            for s in range(2):
                hr, hi = half[s][b]
                term = (ur * hr - ui * hi, ur * hi + ui * hr)
                out[s][a] = term if b == 0 else add_turned(out[s][a], term, 0)
    return out


def link_dagger(gauge, mu, t, half):
    out = [[None] * 3 for _ in range(2)]
    for a in range(3):
        for b in range(3):
            ur = gauge[mu, 0, b * 3 + a, t]
            ui = gauge[mu, 1, b * 3 + a, t]
            for s in range(2):
                hr, hi = half[s][b]
                term = (ur * hr + ui * hi, ur * hi - ui * hr)
                out[s][a] = term if b == 0 else add_turned(out[s][a], term, 0)
    return out


def load_spinor(ref, t):
    return [[(ref[s * 3 + c, t], ref[12 + s * 3 + c, t]) for c in range(3)] for s in range(4)]


def load_half(ref, *lead):
    return [[(ref[(*lead, s * 3 + c)], ref[(*lead, 6 + s * 3 + c)]) for c in range(3)] for s in range(2)]


def store_half(ref, half, *lead):
    for s in range(2):
        for c in range(3):
            ref[(*lead, s * 3 + c)] = half[s][c][0]
            ref[(*lead, 6 + s * 3 + c)] = half[s][c][1]


def map_half(half, change):
    return [[(change(z[0]), change(z[1])) for z in row] for row in half]


def roll(value, shift, axis):
    shift %= value.shape[axis]
    return value if shift == 0 else pltpu.roll(value, shift, axis)


def split_columns(a, b, top):
    return (
        jnp.where(top, a, pltpu.roll(b, BLK, 0)),
        jnp.where(top, pltpu.roll(a, BLK, 0), b),
    )


def kernel(
    counts, bc_ref, slot_ref, src_hbm, it_hbm, ga_hbm, cl_hbm, nu_hbm, co_hbm, out_it, out_res,
    src, itv, ga, cl, nu, co, res, corr, nit, ht, gt, hb, ps, pr, rc, mrows, wbuf, rhs, wr, wz, part, wexp,
    load_sem, send_sem, recv_sem,
):
    T = itv.shape[1]
    loads = []
    for i, (a, b) in enumerate(
        [(it_hbm, itv), (ga_hbm, ga), (src_hbm, src), (cl_hbm, cl), (nu_hbm, nu), (co_hbm, co)]
    ):
        copy = pltpu.make_async_copy(a, b, load_sem.at[i])
        copy.start()
        loads.append(copy)

    names = ("ta", "gz", "xy")
    place = {n: lax.axis_index(n) for n in names}
    ahead = {n: {n: lax.rem(place[n] + 1, counts[n])} for n in names}
    behind = {n: {n: lax.rem(place[n] + counts[n] - 1, counts[n])} for n in names}
    barrier = pltpu.get_barrier_semaphore()
    for n in names:
        for target in (ahead[n], behind[n]):
            pl.semaphore_signal(barrier, inc=1, device_id=target, device_id_type=MESH)
    pl.semaphore_wait(barrier, 6)

    def send(number, source, target, device):
        copy = pltpu.make_async_remote_copy(
            src_ref=source, dst_ref=target, send_sem=send_sem.at[number], recv_sem=recv_sem.at[number],
            device_id=device, device_id_type=MESH,
        )
        copy.start()
        return copy

    row = lax.broadcasted_iota(jnp.int32, (8, 128), 0)
    lane = lax.broadcasted_iota(jnp.int32, (8, 128), 1)
    column_y = lane & (LY - 1)
    sign = [bc_ref[mu].astype(F32) for mu in range(4)]
    last = [jnp.where(place[n] == counts[n] - 1, sign[i], 1.0) for i, n in enumerate(names)]
    first = [jnp.where(place[n] == 0, sign[i], 1.0) for i, n in enumerate(names)]

    def subtract_fine(d, field, base, out, before_local):
        def prepare(t, carry):
            psi = load_spinor(field, t)
            store_half(ht, project(psi, 0, True), d, t)
            store_half(gt, link_dagger(ga, 0, t, project(psi, 0, False)), d, t + 1)
            for mu in (1, 2):
                store_half(hb, project(psi, mu, True), 2 * mu - 2, t)
                store_half(hb, link_dagger(ga, mu, t, project(psi, mu, False)), 2 * mu - 1, t)
            return carry

        lax.fori_loop(0, T, prepare, 0)

        def pack(c, carry):
            z0, z1, x0, x1 = hb[0, 0, c], roll(hb[1, 0, c], 1, 0), hb[2, 0, c], roll(hb[3, 0, c], LY, 1)
            for t in range(1, T):
                z0 = jnp.where(row == t, roll(hb[0, t, c], t, 0), z0)
                z1 = jnp.where(row == t, roll(hb[1, t, c], t + 1, 0), z1)
                mine = (lane // LY) == t
                x0 = jnp.where(mine, roll(hb[2, t, c], LY * t, 1), x0)
                x1 = jnp.where(mine, roll(hb[3, t, c], LY * t + LY, 1), x1)
            ps[d, 0, c] = z0
            ps[d, 1, c] = z1
            ps[d, 2, c] = x0
            ps[d, 3, c] = x1
            return carry

        base_number = d * 6
        copies = [
            send(base_number, ht.at[d, 0], ht.at[d, T], behind["ta"]),
            send(base_number + 1, gt.at[d, T], gt.at[d, 0], ahead["ta"]),
        ]
        lax.fori_loop(0, 12, pack, 0)
        for kind, target in enumerate((behind["gz"], ahead["gz"], behind["xy"], ahead["xy"])):
            copies.append(send(base_number + 2 + kind, ps.at[d, kind], pr.at[d, kind], target))

        before_local()

        def local(t, carry):
            psi = load_spinor(field, t)
            total = [[(jnp.zeros((8, 128), F32), jnp.zeros((8, 128), F32)) for _ in range(3)] for _ in range(4)]

            def up(v):
                return jnp.where(column_y == LY - 1, roll(v, LY - 1, 1) * sign[3], roll(v, -1, 1))

            def down(v):
                return jnp.where(column_y == 0, roll(v, 1 - LY, 1) * sign[3], roll(v, 1, 1))

            rebuild(total, link_times(ga, 3, t, map_half(project(psi, 3, True), up)), 3, True)
            rebuild(total, map_half(link_dagger(ga, 3, t, project(psi, 3, False)), down), 3, False)
            for ch in range(2):
                for i in range(6):
                    s, c = 2 * ch + i // 3, i % 3
                    re, im = psi[s][c][0] * MASS_TERM, psi[s][c][1] * MASS_TERM
                    for j in range(6):
                        vr, vi = psi[2 * ch + j // 3][j % 3]
                        mr, mi = cl[ch, 0, i * 6 + j, t], cl[ch, 1, i * 6 + j, t]
                        re = re + (mr * vr - mi * vi)
                        im = im + (mr * vi + mi * vr)
                    k = s * 3 + c
                    out[k, t] = base[k, t] - re + 0.5 * total[s][c][0]
                    out[12 + k, t] = base[12 + k, t] - im + 0.5 * total[s][c][1]
            return carry

        lax.fori_loop(0, T, local, 0)
        for copy in copies:
            copy.wait()

        def unpack(c, carry):
            z0, z1 = pr[d, 0, c] * last[1], pr[d, 1, c] * first[1]
            x0, x1 = pr[d, 2, c] * last[2], pr[d, 3, c] * first[2]
            for t in range(T):
                hb[0, t, c] = jnp.where(row == 7, roll(z0, 7 - t, 0), roll(hb[0, t, c], -1, 0))
                hb[1, t, c] = jnp.where(row == 0, roll(z1, -t, 0), roll(hb[1, t, c], 1, 0))
                hb[2, t, c] = jnp.where(lane >= 128 - LY, roll(x0, 128 - LY - LY * t, 1), roll(hb[2, t, c], -LY, 1))
                hb[3, t, c] = jnp.where(lane < LY, roll(x1, -LY * t, 1), roll(hb[3, t, c], LY, 1))
            return carry

        lax.fori_loop(0, 12, unpack, 0)

        def finish(t, carry):
            total = [[(jnp.zeros((8, 128), F32), jnp.zeros((8, 128), F32)) for _ in range(3)] for _ in range(4)]
            edge = jnp.where(t == T - 1, last[0], 1.0)
            rebuild(total, link_times(ga, 0, t, map_half(load_half(ht, d, t + 1), lambda v: v * edge)), 0, True)
            low = jnp.where(t == 0, first[0], 1.0)
            rebuild(total, map_half(load_half(gt, d, t), lambda v: v * low), 0, False)
            for mu in (1, 2):
                rebuild(total, link_times(ga, mu, t, load_half(hb, 2 * mu - 2, t)), mu, True)
                rebuild(total, load_half(hb, 2 * mu - 1, t), mu, False)
            for s in range(4):
                for c in range(3):
                    k = s * 3 + c
                    out[k, t] = out[k, t] + 0.5 * total[s][c][0]
                    out[12 + k, t] = out[12 + k, t] + 0.5 * total[s][c][1]
            return carry

        lax.fori_loop(0, T, finish, 0)

    mrows[...] = jnp.zeros(mrows.shape, F32)
    loads[0].wait()
    loads[1].wait()

    def rest():
        loads[2].wait()
        loads[3].wait()

    subtract_fine(0, itv, src, res, rest)

    top = row < BLK

    def to_columns(k, carry):
        for pair in range(2):
            parts = split_columns(res[k, 2 * pair], res[k, 2 * pair + 1], top)
            for col in range(2):
                rc[col, k, pl.ds(8 * pair, 8), :] = parts[col].astype(jnp.bfloat16).astype(F32)
        return carry

    lax.fori_loop(0, 24, to_columns, 0)
    loads[4].wait()
    group = 4
    for col in range(2):
        slot = slot_ref[col]

        def restrict(g, carry):
            re = [jnp.zeros((16, 128), F32) for _ in range(group)]
            im = [jnp.zeros((16, 128), F32) for _ in range(group)]
            for s in range(12):
                fr, fi = rc[col, s], rc[col, 12 + s]
                for j in range(group):
                    nr = nu[slot, 0, g * group + j, s].astype(F32)
                    ni = nu[slot, 1, g * group + j, s].astype(F32)
                    re[j] = re[j] + (nr * fr + ni * fi)
                    im[j] = im[j] + (nr * fi - ni * fr)
            for j in range(group):
                mrows[col, 0, pl.ds(g * group + j, 1), :] = jnp.sum(re[j], axis=0, keepdims=True)
                mrows[col, 1, pl.ds(g * group + j, 1), :] = jnp.sum(im[j], axis=0, keepdims=True)
            return carry

        lax.fori_loop(0, 24 // group, restrict, 0)
    chooser = ((column_y // BLK) == row).astype(F32)
    for col in range(2):
        for ri in range(2):
            value = lax.dot_general(
                chooser, mrows[col, ri], (((1,), (1,)), ((), ())), precision=HIGHEST, preferred_element_type=F32
            )
            rhs[col, ri] = value
            wbuf[0, col, ri] = RELAX_WEIGHT * value
    loads[5].wait()

    nv = co.shape[-1]
    block = 8
    for it in range(CITERS - 1):
        number = 12 + it * 6
        copies = [
            send(number, wbuf.at[it], wr.at[it, 0], behind["ta"]),
            send(number + 1, wbuf.at[it], wr.at[it, 1], ahead["ta"]),
            send(number + 2, wbuf.at[it], wr.at[it, 2], behind["xy"]),
            send(number + 3, wbuf.at[it], wr.at[it, 3], ahead["xy"]),
            send(number + 4, wbuf.at[it, 0], wz.at[it, 0], behind["gz"]),
            send(number + 5, wbuf.at[it, 1], wz.at[it, 1], ahead["gz"]),
        ]

        def products(col, pairs, i, re, im):
            for k, vr, vi in pairs:
                yr, yi = co[k, 0, i, col], co[k, 1, i, col]
                a, b = yr * vr - yi * vi, yr * vi + yi * vr
                re, im = (a, b) if re is None else (re + a, im + b)
            return re, im

        for col in range(2):
            own = [wbuf[it, col, ri] for ri in range(2)]
            other = [wbuf[it, 1 - col, ri, :, :nv] for ri in range(2)]
            pairs = [
                (0, own[0][:, :nv], own[1][:, :nv]),
                (3 if col == 0 else 4, other[0], other[1]),
                (7, roll(own[0], -1, 0)[:, :nv], roll(own[1], -1, 0)[:, :nv]),
                (8, roll(own[0], 1, 0)[:, :nv], roll(own[1], 1, 0)[:, :nv]),
            ]

            def near(g, carry):
                for j in range(block):
                    i = g * block + j
                    re, im = products(col, pairs, i, None, None)
                    part[col, 0, i] = re
                    part[col, 1, i] = im
                return carry

            lax.fori_loop(0, nv // block, near, 0)
        for copy in copies:
            copy.wait()
        for col in range(2):
            pairs = [
                (k, wr[it, d, col, 0, :, :nv], wr[it, d, col, 1, :, :nv])
                for k, d in ((1, 0), (2, 1), (5, 2), (6, 3))
            ]
            far_z = 1 - col
            pairs.append((4 if col == 0 else 3, wz[it, far_z, 0, :, :nv], wz[it, far_z, 1, :, :nv]))

            def far(g, carry):
                new_re, new_im = carry
                for j in range(block):
                    i = g * block + j
                    re, im = products(col, pairs, i, part[col, 0, i], part[col, 1, i])
                    new_re = jnp.where(lane == i, jnp.sum(re, axis=1, keepdims=True), new_re)
                    new_im = jnp.where(lane == i, jnp.sum(im, axis=1, keepdims=True), new_im)
                return new_re, new_im

            zero = jnp.zeros((8, 128), F32)
            applied = lax.fori_loop(0, nv // block, far, (zero, zero))
            for ri in range(2):
                w = wbuf[it, col, ri]
                wbuf[it + 1, col, ri] = w + RELAX_WEIGHT * (rhs[col, ri] - (2.0 * w + applied[ri]))

    for col in range(2):
        for ri in range(2):
            w = wbuf[CITERS - 1, col, ri].astype(jnp.bfloat16).astype(F32)
            wexp[col, ri] = lax.dot_general(
                w, chooser, (((0,), (0,)), ((), ())), precision=HIGHEST, preferred_element_type=F32
            )
    spins = 3
    step = 4
    for col in range(2):
        slot = slot_ref[col]

        def some_spins(q, carry):
            def over(g, totals):
                totals = list(totals)
                for j in range(step):
                    c = g * step + j
                    vr = wexp[col, 0, pl.ds(c, 1), :]
                    vi = wexp[col, 1, pl.ds(c, 1), :]
                    for m in range(spins):
                        nr = nu[slot, 0, c, q * spins + m].astype(F32)
                        ni = nu[slot, 1, c, q * spins + m].astype(F32)
                        totals[2 * m] = totals[2 * m] + (nr * vr - ni * vi)
                        totals[2 * m + 1] = totals[2 * m + 1] + (nr * vi + ni * vr)
                return tuple(totals)

            zero = jnp.zeros((16, 128), F32)
            totals = lax.fori_loop(0, nv // step, over, (zero,) * (2 * spins))
            for m in range(spins):
                rc[col, q * spins + m] = totals[2 * m]
                rc[col, 12 + q * spins + m] = totals[2 * m + 1]
            return carry

        lax.fori_loop(0, 12 // spins, some_spins, 0)

    def from_columns(k, carry):
        for pair in range(2):
            part_0 = rc[0, k, pl.ds(8 * pair, 8), :]
            part_1 = rc[1, k, pl.ds(8 * pair, 8), :]
            values = split_columns(part_0, part_1, top)
            for h in range(2):
                t = 2 * pair + h
                corr[k, t] = values[h]
                nit[k, t] = itv[k, t] + values[h]
        return carry

    lax.fori_loop(0, 24, from_columns, 0)
    store_it = pltpu.make_async_copy(nit, out_it, load_sem.at[6])
    store_it.start()
    subtract_fine(1, corr, res, res, lambda: None)
    store_res = pltpu.make_async_copy(res, out_res, load_sem.at[7])
    store_res.start()
    store_it.wait()
    store_res.wait()


def per_device(counts, source, iterate, gauge_links, clover, bc_sign, null_store, block_slot, coarse_links):
    lattice = source.shape[3:]
    T = lattice[0]
    spinor = (24,) + lattice
    columns = block_slot.size
    nv = null_store.shape[4]
    assert lattice == (BLK, 2 * BLK, BLK * LY) and columns == 2
    nulls = (columns,) + null_store.shape[3:6] + (BLK * BLK, BLK * LY)
    links = jnp.transpose(coarse_links, (0, 1, 2, 4, 5, 6, 7, 3))
    links = links.reshape(links.shape[:3] + (columns,) + links.shape[6:])
    gauge_shape = (4, 2, 9) + lattice
    clover_shape = (2, 2, 36) + lattice
    half = (12,) + lattice[1:]
    tile = lattice[1:]
    smem = pl.BlockSpec(memory_space=pltpu.SMEM)
    hbm = pl.BlockSpec(memory_space=pl.ANY)
    fine = jax.ShapeDtypeStruct(spinor, F32)
    n_copies = 12 + 6 * (CITERS - 1)
    outs = pl.pallas_call(
        functools.partial(kernel, counts),
        out_shape=(fine, fine),
        in_specs=[smem, smem] + [hbm] * 6,
        out_specs=(hbm, hbm),
        scratch_shapes=[
            pltpu.VMEM(spinor, F32),
            pltpu.VMEM(spinor, F32),
            pltpu.VMEM(gauge_shape, F32),
            pltpu.VMEM(clover_shape, F32),
            pltpu.VMEM(nulls, jnp.bfloat16),
            pltpu.VMEM(links.shape, F32),
            pltpu.VMEM(spinor, F32),
            pltpu.VMEM(spinor, F32),
            pltpu.VMEM(spinor, F32),
            pltpu.VMEM((2, T + 1) + half, F32),
            pltpu.VMEM((2, T + 1) + half, F32),
            pltpu.VMEM((4, T) + half, F32),
            pltpu.VMEM((2, 4) + half, F32),
            pltpu.VMEM((2, 4) + half, F32),
            pltpu.VMEM((columns, 24, BLK * BLK, BLK * LY), F32),
            pltpu.VMEM((columns, 2, 128, 128), F32),
            pltpu.VMEM((CITERS, columns, 2) + tile, F32),
            pltpu.VMEM((columns, 2) + tile, F32),
            pltpu.VMEM((CITERS - 1, 4, columns, 2) + tile, F32),
            pltpu.VMEM((CITERS - 1, 2, 2) + tile, F32),
            pltpu.VMEM((columns, 2, nv, 8, nv), F32),
            pltpu.VMEM((columns, 2, 128, 128), F32),
            pltpu.SemaphoreType.DMA((8,)),
            pltpu.SemaphoreType.DMA((n_copies,)),
            pltpu.SemaphoreType.DMA((n_copies,)),
        ],
        compiler_params=pltpu.CompilerParams(
            collective_id=0, has_side_effects=True, vmem_limit_bytes=67_043_328
        ),
    )(
        bc_sign,
        block_slot.reshape(-1),
        source.reshape(spinor),
        iterate.reshape(spinor),
        gauge_links.reshape(gauge_shape),
        clover.reshape(clover_shape),
        null_store.reshape(nulls),
        links,
    )
    return tuple(out.reshape(source.shape) for out in outs)


def solution(mesh):
    placed = (
        P(None, None, None, "ta", "gz", "xy"),
        P(None, None, None, "ta", "gz", "xy"),
        P(None, None, None, None, "ta", "gz", "xy"),
        P(None, None, None, None, "ta", "gz", "xy"),
        P(),
        P("ta", "gz", "xy", None, None, None, None, None, None),
        P("ta", "gz", "xy"),
        P(None, None, None, None, "ta", "gz", "xy", None),
    )
    return jax.shard_map(
        functools.partial(per_device, dict(mesh.shape)),
        mesh=mesh,
        in_specs=placed,
        out_specs=(P(None, None, None, "ta", "gz", "xy"), P(None, None, None, "ta", "gz", "xy")),
        check_vma=False,
    )
```

time: 490 us -> 44.7 us (0.09); the launches traced: 480 us -> 44.4 us
  local copies, waits for them, and re-layouts: 183 us -> 3.53 us
  matrix products: 164 us -> 0 us
  waiting for transfers between devices: 59.2 us -> 0 us
  Pallas kernels: 0 us -> 40.3 us
  starting transfers between devices: 33.2 us -> 0 us
  other arithmetic: 32.3 us -> 0 us
  between operations: 8.81 us -> 0.64 us
    dot_general x78 -> x0, matrix products: 164 us -> none  [the longest x1 84.2 us: prolong_local(): jnp.einsum('tzxpvsabw,qpvtzxw->qstazbxw', null_rows, mixture, preferred_e...]
    select_n x2 -> x0, local copies, waits for them, and re-layouts: 109 us -> none  [per_device(): null_rows = jnp.take(flat_store, block_slot.reshape(-1), axis=0)]
    ppermute x33 -> x0, waiting for transfers between devices: 59.2 us -> none  [the longest x15 29.6 us: padded_2(): lax.ppermute(lax.slice_in_dim(block, 0, width, axis=dim), axis, backward)]
    pallas_call x0 -> x1, Pallas kernels: none -> 40.3 us  [per_device(): pl.pallas_call(functools.partial(kernel, counts), out_shape=(fine, fine),...]
    ppermute x33 -> x0, starting transfers between devices: 33.2 us -> none  [the longest x15 21 us: padded_2(): lax.ppermute(lax.slice_in_dim(block, 0, width, axis=dim), axis, backward)]
    another operation x9 -> x0, local copies, waits for them, and re-layouts: 26 us -> none  [the longest x2 19.6 us: restrict_local(): paired = jnp.stack([shaped, turned])]
    gather x4 -> x0, local copies, waits for them, and re-layouts: 11 us -> none
    mul x137 -> x0, local copies, waits for them, and re-layouts: 10 us -> none  [the longest x68 7.48 us: colour_times(): real_part = real_part + link_re * field_re - link_im * field_im]
  transfers between devices with their start and end apart: 33 -> 0, of which waited for: 25 -> 0; matrix products, arithmetic and copies ran while one was open for 35% -> 0% of each run, Pallas kernels for 0% -> 0%
where the time goes in v1:
time: 44.7 us; the launch traced here: 44.4 us
  Pallas kernels  40.3 us (90%)
  local copies, waits for them, and re-layouts  3.53 us (8%)
  between operations  0.64 us (1%)
    pallas_call x1, Pallas kernels, per_device(): pl.pallas_call(functools.partial(kernel, counts), out_shape=(fine, fine),...  40.3 us
    unnamed x2, local copies, waits for them, and re-layouts  3.53 us

profile of v1, /device:TPU:0, one launch (start us, length us, event | category | flops | bytes accessed | tf_op | source)
XLA Modules:
  0.0 44.4 jit_solution(9721521877749702711)
XLA Ops:
  0.6 40.3 %shard_map.95 = (f32[24,4,8,128]{3,2,1,0:T(8,128)}, f32[24,4,8,128]{3,2,1,0:T(8,128)}) custom-call(s32[4]{0:T(128)} %bc_ref.1, s32[2]{0:T(128)} %bitcast.21, f32[24,4,8,128]{3,2,1,0:T(8,128)} %bitcast.17, f32[24,4,8,128]{3,2,1,0:T(8,128)} %bitcast.18, f32[4,2,9,4,8,128]{5,4,3,2,1,0:T(8,128)} %bitcast.16, f32[2,2,36,4,8,128]{5,4,3,2,1,0:T(8,128)} %bitcast.15, ...), custom_call_target="tpu_custom_call" | custom-call | tf_op jit(solution)/shard_map/pallas_call | solution.py:432
  40.9 1.8 %copy.13 = f32[2,4,3,4,8,128]{5,4,3,2,1,0:T(8,128)} copy(f32[2,4,3,4,8,128]{5,4,3,2,1,0:T(8,128)} %bitcast.20) | data formatting | bytes 786432
  42.7 1.8 %copy.14 = f32[2,4,3,4,8,128]{5,4,3,2,1,0:T(8,128)} copy(f32[2,4,3,4,8,128]{5,4,3,2,1,0:T(8,128)} %bitcast.19) | data formatting | bytes 786432

commit v2 on v1

--- a/solution.py
+++ b/solution.py
@@ -14,6 +14,7 @@
 RELAX_WEIGHT = 0.4
 HIGHEST = lax.Precision.HIGHEST
 MESH = pl.DeviceIdType.MESH
+LANES = 32
 F32 = jnp.float32
 
 UPPER = [((0, 0), (1, 0)), ((0, 3), (1, 1)), ((1, 3), (0, 3)), ((1, 2), (0, 0))]
@@ -107,7 +108,7 @@
 
 def kernel(
     counts, bc_ref, slot_ref, src_hbm, it_hbm, ga_hbm, cl_hbm, nu_hbm, co_hbm, out_it, out_res,
-    src, itv, ga, cl, nu, co, res, corr, nit, ht, gt, hb, ps, pr, rc, mrows, wbuf, rhs, wr, wz, part, wexp,
+    src, itv, ga, cl, nu, co, res, corr, nit, ht, gt, hb, hs, ps, pr, rc, mrows, wbuf, rhs, wr, part, wexp,
     load_sem, send_sem, recv_sem,
 ):
     T = itv.shape[1]
@@ -127,7 +128,6 @@
     for n in names:
         for target in (ahead[n], behind[n]):
             pl.semaphore_signal(barrier, inc=1, device_id=target, device_id_type=MESH)
-    pl.semaphore_wait(barrier, 6)
 
     def send(number, source, target, device):
         copy = pltpu.make_async_remote_copy(
@@ -156,27 +156,30 @@
 
         lax.fori_loop(0, T, prepare, 0)
 
-        def pack(c, carry):
-            z0, z1, x0, x1 = hb[0, 0, c], roll(hb[1, 0, c], 1, 0), hb[2, 0, c], roll(hb[3, 0, c], LY, 1)
-            for t in range(1, T):
-                z0 = jnp.where(row == t, roll(hb[0, t, c], t, 0), z0)
-                z1 = jnp.where(row == t, roll(hb[1, t, c], t + 1, 0), z1)
-                mine = (lane // LY) == t
-                x0 = jnp.where(mine, roll(hb[2, t, c], LY * t, 1), x0)
-                x1 = jnp.where(mine, roll(hb[3, t, c], LY * t + LY, 1), x1)
-            ps[d, 0, c] = z0
-            ps[d, 1, c] = z1
-            ps[d, 2, c] = x0
-            ps[d, 3, c] = x1
-            return carry
-
+        def pack(g, carry):
+            for k in range(4):
+                c = g * 4 + k
+                z0, z1, x0, x1 = hb[0, 0, c], roll(hb[1, 0, c], 1, 0), hb[2, 0, c], roll(hb[3, 0, c], LY, 1)
+                for t in range(1, T):
+                    z0 = jnp.where(row == t, roll(hb[0, t, c], t, 0), z0)
+                    z1 = jnp.where(row == t, roll(hb[1, t, c], t + 1, 0), z1)
+                    mine = (lane // LY) == t
+                    x0 = jnp.where(mine, roll(hb[2, t, c], LY * t, 1), x0)
+                    x1 = jnp.where(mine, roll(hb[3, t, c], LY * t + LY, 1), x1)
+                for kind, value in enumerate((z0, z1, x0, x1)):
+                    ps[d, kind, c] = value
+            return carry
+
+        if d == 0:
+            pl.semaphore_wait(barrier, 6)
         base_number = d * 6
         copies = [
             send(base_number, ht.at[d, 0], ht.at[d, T], behind["ta"]),
             send(base_number + 1, gt.at[d, T], gt.at[d, 0], ahead["ta"]),
         ]
-        lax.fori_loop(0, 12, pack, 0)
-        for kind, target in enumerate((behind["gz"], ahead["gz"], behind["xy"], ahead["xy"])):
+        lax.fori_loop(0, 3, pack, 0)
+        targets = (behind["gz"], ahead["gz"], behind["xy"], ahead["xy"])
+        for kind, target in sorted(enumerate(targets), key=lambda entry: -entry[0]):
             copies.append(send(base_number + 2 + kind, ps.at[d, kind], pr.at[d, kind], target))
 
         before_local()
@@ -211,17 +214,25 @@
         for copy in copies:
             copy.wait()
 
-        def unpack(c, carry):
-            z0, z1 = pr[d, 0, c] * last[1], pr[d, 1, c] * first[1]
-            x0, x1 = pr[d, 2, c] * last[2], pr[d, 3, c] * first[2]
-            for t in range(T):
-                hb[0, t, c] = jnp.where(row == 7, roll(z0, 7 - t, 0), roll(hb[0, t, c], -1, 0))
-                hb[1, t, c] = jnp.where(row == 0, roll(z1, -t, 0), roll(hb[1, t, c], 1, 0))
-                hb[2, t, c] = jnp.where(lane >= 128 - LY, roll(x0, 128 - LY - LY * t, 1), roll(hb[2, t, c], -LY, 1))
-                hb[3, t, c] = jnp.where(lane < LY, roll(x1, -LY * t, 1), roll(hb[3, t, c], LY, 1))
-            return carry
-
-        lax.fori_loop(0, 12, unpack, 0)
+        def unpack(g, carry):
+            for k in range(4):
+                c = g * 4 + k
+                z0, z1 = pr[d, 0, c] * last[1], pr[d, 1, c] * first[1]
+                x0, x1 = pr[d, 2, c] * last[2], pr[d, 3, c] * first[2]
+                new = []
+                for t in range(T):
+                    new.append((
+                        jnp.where(row == 7, roll(z0, 7 - t, 0), roll(hb[0, t, c], -1, 0)),
+                        jnp.where(row == 0, roll(z1, -t, 0), roll(hb[1, t, c], 1, 0)),
+                        jnp.where(lane >= 128 - LY, roll(x0, 128 - LY - LY * t, 1), roll(hb[2, t, c], -LY, 1)),
+                        jnp.where(lane < LY, roll(x1, -LY * t, 1), roll(hb[3, t, c], LY, 1)),
+                    ))
+                for t in range(T):
+                    for kind in range(4):
+                        hs[kind, t, c] = new[t][kind]
+            return carry
+
+        lax.fori_loop(0, 3, unpack, 0)
 
         def finish(t, carry):
             total = [[(jnp.zeros((8, 128), F32), jnp.zeros((8, 128), F32)) for _ in range(3)] for _ in range(4)]
@@ -230,8 +241,8 @@
             low = jnp.where(t == 0, first[0], 1.0)
             rebuild(total, map_half(load_half(gt, d, t), lambda v: v * low), 0, False)
             for mu in (1, 2):
-                rebuild(total, link_times(ga, mu, t, load_half(hb, 2 * mu - 2, t)), mu, True)
-                rebuild(total, load_half(hb, 2 * mu - 1, t), mu, False)
+                rebuild(total, link_times(ga, mu, t, load_half(hs, 2 * mu - 2, t)), mu, True)
+                rebuild(total, load_half(hs, 2 * mu - 1, t), mu, False)
             for s in range(4):
                 for c in range(3):
                     k = s * 3 + c
@@ -277,91 +288,86 @@
                     re[j] = re[j] + (nr * fr + ni * fi)
                     im[j] = im[j] + (nr * fi - ni * fr)
             for j in range(group):
-                mrows[col, 0, pl.ds(g * group + j, 1), :] = jnp.sum(re[j], axis=0, keepdims=True)
-                mrows[col, 1, pl.ds(g * group + j, 1), :] = jnp.sum(im[j], axis=0, keepdims=True)
+                mrows[pl.ds((2 * col) * LANES + g * group + j, 1), :] = jnp.sum(re[j], axis=0, keepdims=True)
+                mrows[pl.ds((2 * col + 1) * LANES + g * group + j, 1), :] = jnp.sum(im[j], axis=0, keepdims=True)
             return carry
 
         lax.fori_loop(0, 24 // group, restrict, 0)
     chooser = ((column_y // BLK) == row).astype(F32)
-    for col in range(2):
-        for ri in range(2):
-            value = lax.dot_general(
-                chooser, mrows[col, ri], (((1,), (1,)), ((), ())), precision=HIGHEST, preferred_element_type=F32
-            )
-            rhs[col, ri] = value
-            wbuf[0, col, ri] = RELAX_WEIGHT * value
+    value = lax.dot_general(
+        chooser, mrows[...], (((1,), (1,)), ((), ())), precision=HIGHEST, preferred_element_type=F32
+    )
+    rhs[...] = value
+    wbuf[0] = RELAX_WEIGHT * value
     loads[5].wait()
 
     nv = co.shape[-1]
     block = 8
+    def pieces(vector, col):
+        return [roll(vector, -LANES * (2 * col + ri), 1)[:, :nv] for ri in range(2)]
+
+    def products(col, pairs, i, re, im):
+        for k, (vr, vi) in pairs:
+            yr, yi = co[k, 0, i, col], co[k, 1, i, col]
+            a, b = yr * vr - yi * vi, yr * vi + yi * vr
+            re, im = (a, b) if re is None else (re + a, im + b)
+        return re, im
+
     for it in range(CITERS - 1):
-        number = 12 + it * 6
-        copies = [
-            send(number, wbuf.at[it], wr.at[it, 0], behind["ta"]),
-            send(number + 1, wbuf.at[it], wr.at[it, 1], ahead["ta"]),
-            send(number + 2, wbuf.at[it], wr.at[it, 2], behind["xy"]),
-            send(number + 3, wbuf.at[it], wr.at[it, 3], ahead["xy"]),
-            send(number + 4, wbuf.at[it, 0], wz.at[it, 0], behind["gz"]),
-            send(number + 5, wbuf.at[it, 1], wz.at[it, 1], ahead["gz"]),
+        targets = [ahead["ta"], behind["ta"], ahead["gz"], behind["gz"], ahead["xy"], behind["xy"]]
+        copies = [None] * 6
+        for d in (4, 5, 0, 1, 2, 3):
+            copies[d] = send(12 + it * 6 + d, wbuf.at[it], wr.at[it, d], targets[d ^ 1])
+        own = wbuf[it]
+        up, down = roll(own, -1, 0), roll(own, 1, 0)
+        copies[2].wait()
+        copies[3].wait()
+        next_z, last_z = wr[it, 2], wr[it, 3]
+        pairs = [
+            [
+                (0, pieces(own, col)),
+                (7, pieces(up, col)),
+                (8, pieces(down, col)),
+                (3, pieces(own, 1) if col == 0 else pieces(next_z, 0)),
+                (4, pieces(own, 0) if col == 1 else pieces(last_z, 1)),
+            ]
+            for col in range(2)
         ]
 
-        def products(col, pairs, i, re, im):
-            for k, vr, vi in pairs:
-                yr, yi = co[k, 0, i, col], co[k, 1, i, col]
-                a, b = yr * vr - yi * vi, yr * vi + yi * vr
-                re, im = (a, b) if re is None else (re + a, im + b)
-            return re, im
-
-        for col in range(2):
-            own = [wbuf[it, col, ri] for ri in range(2)]
-            other = [wbuf[it, 1 - col, ri, :, :nv] for ri in range(2)]
-            pairs = [
-                (0, own[0][:, :nv], own[1][:, :nv]),
-                (3 if col == 0 else 4, other[0], other[1]),
-                (7, roll(own[0], -1, 0)[:, :nv], roll(own[1], -1, 0)[:, :nv]),
-                (8, roll(own[0], 1, 0)[:, :nv], roll(own[1], 1, 0)[:, :nv]),
-            ]
-
-            def near(g, carry):
-                for j in range(block):
-                    i = g * block + j
-                    re, im = products(col, pairs, i, None, None)
+        def near(g, carry):
+            for j in range(block):
+                i = g * block + j
+                for col in range(2):
+                    re, im = products(col, pairs[col], i, None, None)
                     part[col, 0, i] = re
                     part[col, 1, i] = im
-                return carry
-
-            lax.fori_loop(0, nv // block, near, 0)
-        for copy in copies:
-            copy.wait()
-        for col in range(2):
-            pairs = [
-                (k, wr[it, d, col, 0, :, :nv], wr[it, d, col, 1, :, :nv])
-                for k, d in ((1, 0), (2, 1), (5, 2), (6, 3))
-            ]
-            far_z = 1 - col
-            pairs.append((4 if col == 0 else 3, wz[it, far_z, 0, :, :nv], wz[it, far_z, 1, :, :nv]))
-
-            def far(g, carry):
-                new_re, new_im = carry
-                for j in range(block):
-                    i = g * block + j
-                    re, im = products(col, pairs, i, part[col, 0, i], part[col, 1, i])
-                    new_re = jnp.where(lane == i, jnp.sum(re, axis=1, keepdims=True), new_re)
-                    new_im = jnp.where(lane == i, jnp.sum(im, axis=1, keepdims=True), new_im)
-                return new_re, new_im
-
-            zero = jnp.zeros((8, 128), F32)
-            applied = lax.fori_loop(0, nv // block, far, (zero, zero))
-            for ri in range(2):
-                w = wbuf[it, col, ri]
-                wbuf[it + 1, col, ri] = w + RELAX_WEIGHT * (rhs[col, ri] - (2.0 * w + applied[ri]))
-
-    for col in range(2):
-        for ri in range(2):
-            w = wbuf[CITERS - 1, col, ri].astype(jnp.bfloat16).astype(F32)
-            wexp[col, ri] = lax.dot_general(
-                w, chooser, (((0,), (0,)), ((), ())), precision=HIGHEST, preferred_element_type=F32
-            )
+            return carry
+
+        lax.fori_loop(0, nv // block, near, 0)
+        for d in (0, 1, 4, 5):
+            copies[d].wait()
+        far_pairs = [
+            [(k, pieces(wr[it, d], col)) for k, d in ((1, 0), (2, 1), (5, 4), (6, 5))] for col in range(2)
+        ]
+
+        def far(g, applied):
+            for j in range(block):
+                i = g * block + j
+                for col in range(2):
+                    sums = products(col, far_pairs[col], i, part[col, 0, i], part[col, 1, i])
+                    for ri in range(2):
+                        whole = jnp.sum(sums[ri], axis=1, keepdims=True)
+                        applied = jnp.where(lane == LANES * (2 * col + ri) + i, whole, applied)
+            return applied
+
+        applied = lax.fori_loop(0, nv // block, far, jnp.zeros((8, 128), F32))
+        w = wbuf[it]
+        wbuf[it + 1] = w + RELAX_WEIGHT * (rhs[...] - (2.0 * w + applied))
+
+    w = wbuf[CITERS - 1].astype(jnp.bfloat16).astype(F32)
+    wexp[...] = lax.dot_general(
+        w, chooser, (((0,), (0,)), ((), ())), precision=HIGHEST, preferred_element_type=F32
+    )
     spins = 3
     step = 4
     for col in range(2):
@@ -372,8 +378,8 @@
                 totals = list(totals)
                 for j in range(step):
                     c = g * step + j
-                    vr = wexp[col, 0, pl.ds(c, 1), :]
-                    vi = wexp[col, 1, pl.ds(c, 1), :]
+                    vr = wexp[pl.ds(2 * col * LANES + c, 1), :]
+                    vi = wexp[pl.ds((2 * col + 1) * LANES + c, 1), :]
                     for m in range(spins):
                         nr = nu[slot, 0, c, q * spins + m].astype(F32)
                         ni = nu[slot, 1, c, q * spins + m].astype(F32)
@@ -409,6 +415,19 @@
     store_res.start()
     store_it.wait()
     store_res.wait()
+
+
+def hand_over(it_in, res_in, it_out, res_out, it_mid, res_mid, sem):
+    ways = [(it_in, it_mid, it_out), (res_in, res_mid, res_out)]
+    inward = [pltpu.make_async_copy(a, b, sem.at[i]) for i, (a, b, _) in enumerate(ways)]
+    outward = [pltpu.make_async_copy(b, c, sem.at[2 + i]) for i, (_, b, c) in enumerate(ways)]
+    for copy in inward:
+        copy.start()
+    for first, second in zip(inward, outward):
+        first.wait()
+        second.start()
+    for copy in outward:
+        copy.wait()
 
 
 def per_device(counts, source, iterate, gauge_links, clover, bc_sign, null_store, block_slot, coarse_links):
@@ -432,7 +451,7 @@
     outs = pl.pallas_call(
         functools.partial(kernel, counts),
         out_shape=(fine, fine),
-        in_specs=[smem, smem] + [hbm] * 6,
+        in_specs=[smem, smem] + [pl.BlockSpec(memory_space=pltpu.HBM)] * 6,
         out_specs=(hbm, hbm),
         scratch_shapes=[
             pltpu.VMEM(spinor, F32),
@@ -447,16 +466,16 @@
             pltpu.VMEM((2, T + 1) + half, F32),
             pltpu.VMEM((2, T + 1) + half, F32),
             pltpu.VMEM((4, T) + half, F32),
+            pltpu.VMEM((4, T) + half, F32),
             pltpu.VMEM((2, 4) + half, F32),
             pltpu.VMEM((2, 4) + half, F32),
             pltpu.VMEM((columns, 24, BLK * BLK, BLK * LY), F32),
-            pltpu.VMEM((columns, 2, 128, 128), F32),
-            pltpu.VMEM((CITERS, columns, 2) + tile, F32),
-            pltpu.VMEM((columns, 2) + tile, F32),
-            pltpu.VMEM((CITERS - 1, 4, columns, 2) + tile, F32),
-            pltpu.VMEM((CITERS - 1, 2, 2) + tile, F32),
+            pltpu.VMEM((128, 128), F32),
+            pltpu.VMEM((CITERS,) + tile, F32),
+            pltpu.VMEM(tile, F32),
+            pltpu.VMEM((CITERS - 1, 6) + tile, F32),
             pltpu.VMEM((columns, 2, nv, 8, nv), F32),
-            pltpu.VMEM((columns, 2, 128, 128), F32),
+            pltpu.VMEM((128, 128), F32),
             pltpu.SemaphoreType.DMA((8,)),
             pltpu.SemaphoreType.DMA((n_copies,)),
             pltpu.SemaphoreType.DMA((n_copies,)),
@@ -474,6 +493,14 @@
         null_store.reshape(nulls),
         links,
     )
+    outs = pl.pallas_call(
+        hand_over,
+        out_shape=(fine, fine),
+        in_specs=[hbm, hbm],
+        out_specs=(pl.BlockSpec(memory_space=pltpu.HBM),) * 2,
+        scratch_shapes=[pltpu.VMEM(spinor, F32), pltpu.VMEM(spinor, F32), pltpu.SemaphoreType.DMA((4,))],
+        compiler_params=pltpu.CompilerParams(vmem_limit_bytes=67_043_328),
+    )(*outs)
     return tuple(out.reshape(source.shape) for out in outs)
 
 

time: 44.7 us -> 38.4 us (0.86)
  local copies, waits for them, and re-layouts: 3.53 us -> 0 us
  Pallas kernels: 40.3 us -> 37.6 us
    pallas_call x1, Pallas kernels: 40.3 us -> 35.7 us  [per_device(): pl.pallas_call(functools.partial(kernel, counts), out_shape=(fine, fine),...]
    unnamed x2 -> x0, local copies, waits for them, and re-layouts: 3.53 us -> none
    pallas_call x0 -> x1, Pallas kernels: none -> 1.91 us  [per_device(): pl.pallas_call(hand_over, out_shape=(fine, fine), in_specs=[hbm, hbm], ou...]
where the time goes in v2:
time: 38.4 us; the launch traced here: 38.3 us
  Pallas kernels  37.6 us (98%)
  between operations  0.64 us (2%)
    pallas_call x1, Pallas kernels, per_device(): pl.pallas_call(functools.partial(kernel, counts), out_shape=(fine, fine),...  35.7 us
    pallas_call x1, Pallas kernels, per_device(): pl.pallas_call(hand_over, out_shape=(fine, fine), in_specs=[hbm, hbm], ou...  1.91 us

profile of v2, /device:TPU:0, one launch (start us, length us, event | category | flops | bytes accessed | tf_op | source)
XLA Modules:
  0.0 38.3 jit_solution(6859563473744996010)
XLA Ops:
  0.6 35.7 %shard_map.95 = (f32[24,4,8,128]{3,2,1,0:T(8,128)}, f32[24,4,8,128]{3,2,1,0:T(8,128)}) custom-call(s32[4]{0:T(128)} %bc_ref.1, s32[2]{0:T(128)} %bitcast.19, f32[24,4,8,128]{3,2,1,0:T(8,128)} %bitcast.17, f32[24,4,8,128]{3,2,1,0:T(8,128)} %bitcast.18, f32[4,2,9,4,8,128]{5,4,3,2,1,0:T(8,128)} %bitcast.16, f32[2,2,36,4,8,128]{5,4,3,2,1,0:T(8,128)} %bitcast.15, ...), custom_call_target="tpu_custom_call" | custom-call | tf_op jit(solution)/shard_map/pallas_call | solution.py:451
  36.4 1.9 %shard_map.96 = (f32[24,4,8,128]{3,2,1,0:T(8,128)}, f32[24,4,8,128]{3,2,1,0:T(8,128)}) custom-call(f32[24,4,8,128]{3,2,1,0:T(8,128)} %get-tuple-element.6.it_in, f32[24,4,8,128]{3,2,1,0:T(8,128)} %get-tuple-element.7.res_in), custom_call_target="tpu_custom_call" | custom-call | tf_op jit(solution)/shard_map/pallas_call | solution.py:496
